TPU v7x, 32 devices: a whole 2x2x4 slice. The times are simulated.
32 devices in a mesh: gz: 4 (over y, x), gy: 8 (over z, core).
Axes of the slice: x: 2, y: 2, z: 4, core: 2. Of those that a mesh axis runs over, the one named last changes fastest.
Arguments:
- grid_grad: float32 [64, 128, 512], P('gz', 'gy'), may hold values from -6 to 6
- cells: int32 [3, 65536], P(None, ('gz', 'gy')), may hold values from 0 to 511, as said below
- offsets: int32 [3, 65536], P(None, ('gz', 'gy')), may hold values from 0 to 1023
- owners: int32 [65536, 1], P(('gz', 'gy')), may hold values from 0 to 31; in each aligned block of 2048 rows (0 to 2047, 2048 to 4095, ...) at most 128 rows name the same one
- slots: int32 [65536], P(('gz', 'gy')), may hold values from 0 to 2047
Outputs:
- pos_grad: float32 [3, 65536], P(None, ('gz', 'gy'))
Inputs may be any that keep to these rules, and one draw needn't show every extreme that they name: `cells`: the row's cell lies in the mesh block of the device that holds the row: along z in [gz * 16, gz * 16 + 16), along y in [gy * 16, gy * 16 + 16), where gz, gy are that device's indices. `owners`: owners are linear device indices gz * 8 + gy. Among the rows of one device, no owner is named by more than 128 rows; some owner is named by exactly 128.
All inputs are finite; a program needn't handle non-finite values.
Results may differ from a plain program's by a relative error of at most 0.0003.
Values sent between devices are 32-bit elements; how exact they have to be, the bound alone decides.
A program may use at most 64 MiB of HBM per device.

v0:
```python
import jax
import jax.numpy as jnp
from jax import lax
from jax.experimental import pallas as pl
from jax.experimental.pallas import tpu as pltpu
from jax.sharding import PartitionSpec as P

MESH = pl.DeviceIdType.MESH
BF = jnp.bfloat16
F32 = jnp.float32
LANES = 128


def iota(shape, axis):
    return lax.broadcasted_iota(jnp.int32, shape, axis)


def hot(mask):
    return jnp.where(mask, 1.0, 0.0).astype(BF)


def split(value):
    high = value.astype(BF)
    low = (value - high.astype(F32)).astype(BF)
    return high, low


def dot_nn(a, b):
    return lax.dot_general(a, b, (((1,), (0,)), ((), ())), preferred_element_type=F32)


def dot_nt(a, b):
    return lax.dot_general(a, b, (((1,), (1,)), ((), ())), preferred_element_type=F32)


def with_diff(rows):
    size_x = rows.shape[1]
    diff = pltpu.roll(rows, size_x - 1, 1) - rows
    return jnp.concatenate([*split(rows), *split(diff)], axis=0)


def over(count, step, carry):
    if count == 1:
        return step(0, carry)
    return lax.fori_loop(0, count, step, carry)


def kernel(
    grid_ref, cells_ref, offsets_ref, owners_ref, slots_ref, recv_s,
    cells, offsets, owners, slots, grid_v, row_s, corner_s, halo_z, halo_y, halo_c, mesh_s, hot_s, acc_s, rank_s, vals_s,
    send_s, load_sem, own_sem, halo_send, halo_recv, all_send, all_recv,
):
    count_z, count_y = lax.axis_size("gz"), lax.axis_size("gy")
    devices = count_z * count_y
    gz, gy = lax.axis_index("gz"), lax.axis_index("gy")
    me = gz * count_y + gy
    size_z, size_y, size_x = grid_ref.shape
    rows = cells.shape[1]
    chunk = min(256, rows)
    chunks = rows // chunk
    group = min(32, devices)
    groups = devices // group
    slab = size_z * size_y

    loads = []
    for i, (source, target) in enumerate((
        (owners_ref, owners), (grid_ref, grid_v), (cells_ref, cells),
        (offsets_ref, offsets), (slots_ref, slots),
    )):
        loads.append(pltpu.make_async_copy(source, target, load_sem.at[i]))
        loads[-1].start()
    barrier = pltpu.get_barrier_semaphore()

    def each_other(act):
        few = devices <= 64

        def along_y(to_z, first):
            def step(shift, carry):
                act(to_z, lax.rem(gy + shift, count_y))
                return carry
            lax.fori_loop(first, count_y, step, 0, unroll=few)

        def step_z(shift, carry):
            along_y(lax.rem(gz + shift, count_z), 0)
            return carry
        lax.fori_loop(1, count_z, step_z, 0, unroll=few)
        along_y(gz, 1)

    def greet(to_z, to_y):
        pl.semaphore_signal(barrier, inc=1, device_id=(to_z, to_y), device_id_type=MESH)

    each_other(greet)

    loads[0].wait()
    owner = owners[...]
    before = hot(iota((chunk, chunk), 0) < iota((chunk, chunk), 1))

    def rank_group(g, ranks):
        mine = jnp.where(iota((group, rows), 0) + g * group == owner, 1.0, 0.0)
        pieces = [mine[:, c * chunk:(c + 1) * chunk] for c in range(chunks)]
        inside = dot_nn(jnp.concatenate(pieces, axis=0).astype(BF), before)
        start = jnp.zeros((group, 1), F32)
        found = []
        for c in range(chunks):
            where = inside[c * group:(c + 1) * group] + start
            found.append(jnp.sum(pieces[c] * where, axis=0, keepdims=True))
            start = start + jnp.sum(pieces[c], axis=1, keepdims=True)
        return ranks + jnp.concatenate(found, axis=1)

    ranks = over(groups, rank_group, jnp.zeros((1, rows), F32))
    rank_s[...] = hot(iota((LANES, rows), 0) == ranks.astype(jnp.int32))

    loads[1].wait()
    row_s[...] = grid_v[:, 0, :]
    corner_s[...] = grid_v[0, 0:1, :]
    mesh_s[...] = with_diff(grid_v[...].reshape(slab, size_x))

    for copy in loads[2:]:
        copy.wait()

    def place(j):
        span = pl.ds(j * chunk, chunk)
        cell = cells[:, span]
        frac = (offsets[:, span].astype(F32) + 0.5) / 1024.0
        return (span, cell[0:1] - gz * size_z, cell[1:2] - gy * size_y, cell[2:3],
                frac[0:1], frac[1:2], frac[2:3])

    def main_chunk(j):
        span, cz, cy, cx, fz, fy, fx = place(j)
        onehot = hot(iota((size_x, chunk), 0) == cx)
        hot_s[:, span] = onehot
        prod = dot_nn(mesh_s[...], onehot)
        cz, fz = jnp.broadcast_to(cz, (8, chunk)), jnp.broadcast_to(fz, (8, chunk))
        gz0 = 1.0 - fz
        tiles = size_y // 8
        total = [[jnp.zeros((8, chunk), F32) for _ in range(tiles)] for _ in range(4)]
        for z in range(size_z):
            lower, upper = cz == z, cz == z - 1
            weight = jnp.where(lower, gz0, jnp.where(upper, fz, 0.0))
            diff = jnp.where(lower, -1.0, jnp.where(upper, 1.0, 0.0))
            for t in range(tiles):
                first = z * size_y + 8 * t
                at = [prod[q * slab + first:q * slab + first + 8] for q in range(4)]
                value, slope = at[0] + at[1], at[2] + at[3]
                total[0][t] += weight * value
                total[1][t] += diff * value
                total[2][t] += weight * slope
                total[3][t] += diff * slope
        for q in range(4):
            acc_s[q, :, span] = jnp.concatenate(total[q], axis=0)

    part = size_y + size_z + 8

    def halo_chunk(j, ghost):
        span, cz, cy, cx, fz, fy, fx = place(j)
        prod = dot_nn(ghost, hot_s[:, span])
        value = prod[:part] + prod[part:2 * part]
        slope = prod[2 * part:3 * part] + prod[3 * part:]
        top_z, top_y = cz == size_z - 1, cy == size_y - 1
        wz_top, dz_top = jnp.where(top_z, fz, 0.0), jnp.where(top_z, 1.0, 0.0)
        wy_top, dy_top = jnp.where(top_y, fy, 0.0), jnp.where(top_y, 1.0, 0.0)
        a_w = acc_s[0, :, span] + wz_top * value[:size_y]
        a_d = acc_s[1, :, span] + dz_top * value[:size_y]
        b_w = acc_s[2, :, span] + wz_top * slope[:size_y]
        b_d = acc_s[3, :, span] + dz_top * slope[:size_y]
        place_y = iota((size_y, chunk), 0)
        lower, upper = place_y == cy, place_y == cy + 1
        w_y = jnp.where(lower, 1.0 - fy, jnp.where(upper, fy, 0.0))
        d_y = jnp.where(lower, -1.0, jnp.where(upper, 1.0, 0.0))
        grad_z = jnp.sum((a_d + fx * b_d) * w_y, axis=0, keepdims=True)
        grad_y = jnp.sum((a_w + fx * b_w) * d_y, axis=0, keepdims=True)
        grad_x = jnp.sum(b_w * w_y, axis=0, keepdims=True)
        place_z = iota((size_z, chunk), 0)
        lower, upper = place_z == cz, place_z == cz + 1
        w_z = jnp.where(lower, 1.0 - fz, jnp.where(upper, fz, 0.0))
        d_z = jnp.where(lower, -1.0, jnp.where(upper, 1.0, 0.0))
        side = slice(size_y, size_y + size_z)
        corner = slice(size_y + size_z, size_y + size_z + 1)
        read = value[side] + fx * slope[side]
        read_c = value[corner] + fx * slope[corner]
        h_w = jnp.sum(read * w_z, axis=0, keepdims=True) + read_c * wz_top
        h_d = jnp.sum(read * d_z, axis=0, keepdims=True) + read_c * dz_top
        h_x = jnp.sum(slope[side] * w_z, axis=0, keepdims=True) + slope[corner] * wz_top
        record = (slots[:, span] + 1).astype(F32)
        vals_s[:, span] = jnp.concatenate(
            [grad_z + wy_top * h_d, grad_y + dy_top * h_w, grad_x + wy_top * h_x, record] * 2, axis=0)

    early = chunks // 4
    for j in range(early):
        main_chunk(j)
    pl.semaphore_wait(barrier, devices - 1)
    below_z = lax.rem(gz + count_z - 1, count_z)
    below_y = lax.rem(gy + count_y - 1, count_y)
    halos = []
    for i, (source, target, device) in enumerate((
        (corner_s, halo_c, (below_z, below_y)),
        (grid_ref.at[0], halo_z, (below_z, gy)),
        (row_s, halo_y, (gz, below_y)),
    )):
        halos.append(pltpu.make_async_remote_copy(
            src_ref=source, dst_ref=target, send_sem=halo_send.at[i], recv_sem=halo_recv.at[i],
            device_id=device, device_id_type=MESH,
        ))
        halos[-1].start()

    for j in range(early, chunks):
        main_chunk(j)
    for copy in halos:
        copy.wait()
    ghost = with_diff(jnp.concatenate(
        [halo_z[...], halo_y[...], jnp.broadcast_to(halo_c[...], (8, size_x))], axis=0))
    for j in range(chunks):
        halo_chunk(j, ghost)

    def pack_group(g, carry):
        wide = 4 * group
        whose = lax.shift_right_logical(iota((wide, rows), 0), 2) + g * group
        values = jnp.concatenate([vals_s[...]] * (wide // 8), axis=0)
        high, low = split(jnp.where(whose == owner, values, 0.0))
        packed = dot_nt(high, rank_s[...]) + dot_nt(low, rank_s[...])
        for d in range(group):
            send_s[g * group + d] = packed[4 * d:4 * d + 4]
        return carry

    over(groups, pack_group, 0)

    def exchange(source, target, device):
        return pltpu.make_async_remote_copy(
            src_ref=source, dst_ref=target, send_sem=all_send, recv_sem=all_recv,
            device_id=device, device_id_type=MESH,
        )

    own = pltpu.make_async_copy(send_s.at[me], recv_s.at[me], own_sem)

    def post(to_z, to_y):
        other = to_z * count_y + to_y
        exchange(send_s.at[other], recv_s.at[me], (to_z, to_y)).start()

    each_other(post)
    own.start()
    own.wait()
    others = pl.ds(0, devices - 1)
    exchange(send_s.at[others], recv_s.at[others], (below_z, below_y)).wait()


def scatter(recv_s, out):
    devices, rows = recv_s.shape[0], out.shape[1]
    group = min(32, devices)
    groups = devices // group
    highs = rows // LANES

    def add_group(g, total):
        block = jnp.concatenate([recv_s[g * group + d] for d in range(group)], axis=1)
        record = block[3:4].astype(jnp.int32) - 1
        high_at = lax.shift_right_arithmetic(record, 7)
        low_at = lax.bitwise_and(record, LANES - 1)
        width = block.shape[1]
        low_hot = hot(iota((LANES, width), 0) == low_at)
        values = jnp.concatenate([block] * highs, axis=0)
        which = lax.shift_right_logical(iota((4 * highs, width), 0), 2)
        both = jnp.concatenate(split(jnp.where(which == high_at, values, 0.0)), axis=0)
        added = dot_nt(both, low_hot)
        return total + added[:4 * highs] + added[4 * highs:]

    total = over(groups, add_group, jnp.zeros((4 * highs, LANES), F32))
    for h in range(highs):
        out[:, h * LANES:(h + 1) * LANES] = total[4 * h:4 * h + 3]


def body(grid_grad, cells, offsets, owners, slots):
    size_z, size_y, size_x = grid_grad.shape
    rows = cells.shape[1]
    devices = lax.axis_size("gz") * lax.axis_size("gy")
    vmem = pl.BlockSpec(memory_space=pltpu.VMEM)
    hbm = pl.BlockSpec(memory_space=pltpu.HBM)
    received = pl.pallas_call(
        kernel,
        out_shape=jax.ShapeDtypeStruct((devices, 4, LANES), F32),
        in_specs=[hbm] * 5,
        out_specs=hbm,
        scratch_shapes=[
            pltpu.VMEM((3, rows), jnp.int32),
            pltpu.VMEM((3, rows), jnp.int32),
            pltpu.VMEM((1, rows), jnp.int32),
            pltpu.VMEM((1, rows), jnp.int32),
            pltpu.VMEM((size_z, size_y, size_x), F32),
            pltpu.VMEM((size_z, size_x), F32),
            pltpu.VMEM((1, size_x), F32),
            pltpu.VMEM((size_y, size_x), F32),
            pltpu.VMEM((size_z, size_x), F32),
            pltpu.VMEM((1, size_x), F32),
            pltpu.VMEM((4 * size_z * size_y, size_x), BF),
            pltpu.VMEM((size_x, rows), BF),
            pltpu.VMEM((4, size_y, rows), F32),
            pltpu.VMEM((LANES, rows), BF),
            pltpu.VMEM((8, rows), F32),
            pltpu.VMEM((devices, 4, LANES), F32),
            pltpu.SemaphoreType.DMA((5,)),
            pltpu.SemaphoreType.DMA,
            pltpu.SemaphoreType.DMA((3,)),
            pltpu.SemaphoreType.DMA((3,)),
            pltpu.SemaphoreType.DMA,
            pltpu.SemaphoreType.DMA,
        ],
        compiler_params=pltpu.CompilerParams(collective_id=0, has_side_effects=True, vmem_limit_bytes=60 * 1024 * 1024),
        name="cic",
    )(grid_grad, cells, offsets, owners.reshape(1, rows), slots.reshape(1, rows))
    return pl.pallas_call(
        scatter,
        out_shape=jax.ShapeDtypeStruct((3, rows), F32),
        in_specs=[vmem],
        out_specs=vmem,
        compiler_params=pltpu.CompilerParams(vmem_limit_bytes=60 * 1024 * 1024),
        name="scatter",
    )(received)


def solution(mesh):
    placed = (
        P("gz", "gy", None),
        P(None, ("gz", "gy")),
        P(None, ("gz", "gy")),
        P(("gz", "gy"), None),
        P(("gz", "gy")),
    )
    return jax.shard_map(
        body, mesh=mesh, in_specs=placed, out_specs=P(None, ("gz", "gy")), check_vma=False
    )
```

profile of v0, /device:TPU:0, one launch (start us, length us, event | category | flops | bytes accessed | tf_op | source)
XLA Modules:
  0.0 18.5 jit_solution(202153714551295690)
XLA Ops:
  0.0 16.4 %cic.1.recv_s = f32[32,4,128]{2,1,0:T(4,128)} custom-call(f32[16,16,512]{2,1,0:T(8,128)} %grid_ref.1, s32[3,2048]{1,0:T(4,128)} %cells_ref.1, s32[3,2048]{1,0:T(4,128)} %offsets_ref.1, s32[1,2048]{1,0:T(1,128)} %bitcast.2, s32[1,2048]{1,0:T(1,128)} %bitcast.3), custom_call_target="tpu_custom_call" | custom-call | tf_op jit(solution)/shard_map/cic/pallas_call | solution.py:276
  16.4 2.0 %scatter.1 = f32[3,2048]{1,0:T(4,128)} custom-call(f32[32,4,128]{2,1,0:T(4,128)} %cic.1.recv_s), custom_call_target="tpu_custom_call" | custom-call | tf_op jit(solution)/shard_map/scatter/pallas_call | solution.py:308
where the time goes:
time: 18.7 us; the launch traced here: 18.5 us
  Pallas kernels  18.5 us (99%)
    pallas_call x1, Pallas kernels, body(): pl.pallas_call(kernel, out_shape=jax.ShapeDtypeStruct((devices, 4, LANES)...  16.4 us
    pallas_call x1, Pallas kernels, body(): pl.pallas_call(scatter, out_shape=jax.ShapeDtypeStruct((3, rows), F32), i...  2.03 us

commit v1 on v0

v1 whole, which is shorter than its diff:
```python
import jax
import jax.numpy as jnp
from jax import lax
from jax.experimental import pallas as pl
from jax.experimental.pallas import tpu as pltpu
from jax.sharding import PartitionSpec as P

MESH = pl.DeviceIdType.MESH
BF = jnp.bfloat16
F32 = jnp.float32
LANES = 128


def iota(shape, axis):
    return lax.broadcasted_iota(jnp.int32, shape, axis)


def hot(mask):
    return jnp.where(mask, 1.0, 0.0).astype(BF)


def split(value):
    high = value.astype(BF)
    low = (value - high.astype(F32)).astype(BF)
    return high, low


def dot_nn(a, b):
    return lax.dot_general(a, b, (((1,), (0,)), ((), ())), preferred_element_type=F32)


def dot_nt(a, b):
    return lax.dot_general(a, b, (((1,), (1,)), ((), ())), preferred_element_type=F32)


def with_diff(rows):
    size_x = rows.shape[1]
    diff = pltpu.roll(rows, size_x - 1, 1) - rows
    return jnp.concatenate([*split(rows), *split(diff)], axis=0)


def thirds(value):
    high, rest = split(value)
    return high, rest, (value - high.astype(F32) - rest.astype(F32)).astype(BF)


def over(count, step, carry):
    if count == 1:
        return step(0, carry)
    return lax.fori_loop(0, count, step, carry)


def kernel(
    grid_ref, cells_ref, offsets_ref, owners_ref, slots_ref, out,
    cells, offsets, owners, slots, grid_v, row_s, halo_z, halo_y, mesh_s, low_x, base_s, rank_s, mine_s, early_s, later_s,
    early_r, later_r, place_s, high_s, load_sem, halo_send, halo_recv, early_send, early_recv, later_send, later_recv,
):
    count_z, count_y = lax.axis_size("gz"), lax.axis_size("gy")
    devices = count_z * count_y
    gz, gy = lax.axis_index("gz"), lax.axis_index("gy")
    me = gz * count_y + gy
    size_z, size_y, size_x = grid_ref.shape
    rows = cells.shape[1]
    chunk = min(256, rows)
    chunks = rows // chunk
    spans = [pl.ds(j * chunk, chunk) for j in range(chunks)]
    group = min(32, devices)
    groups = devices // group
    slab = size_z * size_y
    pieces_x = size_x // LANES
    fold = low_x.shape[0]
    folds = size_x // fold
    highs = rows // LANES

    loads = []
    for i, (source, target) in enumerate((
        (owners_ref, owners), (grid_ref, grid_v), (cells_ref, cells),
        (offsets_ref, offsets), (slots_ref, slots),
    )):
        loads.append(pltpu.make_async_copy(source, target, load_sem.at[i]))
        loads[-1].start()
    barrier = pltpu.get_barrier_semaphore()

    def each_other(act):
        few = devices <= 64

        def along_y(to_z, first):
            def step(shift, carry):
                act(to_z, lax.rem(gy + shift, count_y))
                return carry
            lax.fori_loop(first, count_y, step, 0, unroll=few)

        def step_z(shift, carry):
            along_y(lax.rem(gz + shift, count_z), 0)
            return carry
        along_y(gz, 1)
        lax.fori_loop(1, count_z, step_z, 0, unroll=few)

    def greet(to_z, to_y):
        pl.semaphore_signal(barrier, inc=1, device_id=(to_z, to_y), device_id_type=MESH)

    each_other(greet)

    for copy in loads:
        copy.wait()
    row_s[...] = grid_v[:, 0, :]
    mesh_s[...] = with_diff(grid_v[...].reshape(slab, size_x))
    corner = grid_v[0, 0:1, :]

    def place(span):
        cell = cells[:, span]
        frac = (offsets[:, span].astype(F32) + 0.5) / 1024.0
        return (cell[0:1] - gz * size_z, cell[1:2] - gy * size_y, cell[2:3],
                frac[0:1], frac[1:2], frac[2:3])

    def weights(size, cell, frac):
        at = iota((size, cell.shape[1]), 0)
        lower, upper = at == cell, at == cell + 1
        return (jnp.where(lower, 1.0 - frac, jnp.where(upper, frac, 0.0)),
                jnp.where(lower, -1.0, jnp.where(upper, 1.0, 0.0)))

    def by_four(first, second, third, fourth):
        part = lax.bitwise_and(iota((8, first.shape[1]), 0), 3)
        return jnp.where(part == 0, first, jnp.where(part == 1, second, jnp.where(part == 2, third, fourth)))

    def main_chunk(span):
        cz, cy, cx, fz, fy, fx = place(span)
        prod = dot_nn(mesh_s[...], hot(iota((size_x, chunk), 0) == cx))
        low_x[:, span] = hot(iota((fold, chunk), 0) == lax.bitwise_and(cx, fold - 1))
        z_at, z_frac = jnp.broadcast_to(cz, (8, chunk)), jnp.broadcast_to(fz, (8, chunk))
        gz0 = 1.0 - z_frac
        tiles = size_y // 8
        total = [[jnp.zeros((8, chunk), F32) for _ in range(tiles)] for _ in range(4)]
        for z in range(size_z):
            lower, upper = z_at == z, z_at == z - 1
            weight = jnp.where(lower, gz0, jnp.where(upper, z_frac, 0.0))
            diff = jnp.where(lower, -1.0, jnp.where(upper, 1.0, 0.0))
            for t in range(tiles):
                first = z * size_y + 8 * t
                at = [prod[q * slab + first:q * slab + first + 8] for q in range(4)]
                value, slope = at[0] + at[1], at[2] + at[3]
                total[0][t] += weight * value
                total[1][t] += diff * value
                total[2][t] += weight * slope
                total[3][t] += diff * slope
        a_w, a_d, b_w, b_d = (jnp.concatenate(t, axis=0) for t in total)
        w_y, d_y = weights(size_y, cy, fy)
        base_s[0:1, span] = jnp.sum((a_d + fx * b_d) * w_y, axis=0, keepdims=True)
        base_s[1:2, span] = jnp.sum((a_w + fx * b_w) * d_y, axis=0, keepdims=True)
        base_s[2:3, span] = jnp.sum(b_w * w_y, axis=0, keepdims=True)

    def top(cell, frac, size):
        at_top = cell == size - 1
        return jnp.where(at_top, frac, 0.0), jnp.where(at_top, 1.0, 0.0)

    def folded(planes):
        table = jnp.concatenate([with_diff(plane) for plane in planes], axis=0)
        return jnp.concatenate([table[:, f * fold:(f + 1) * fold] for f in range(folds)], axis=0)

    def summed(found, fx, w, d):
        size = found.shape[0] // 4
        value, slope = found[:size] + found[size:2 * size], found[2 * size:3 * size] + found[3 * size:]
        read = value + fx * slope
        return [jnp.sum(each, axis=0, keepdims=True) for each in (w * read, d * read, w * slope)]

    def with_halos(table, span):
        cz, cy, cx, fz, fy, fx = place(span)
        prod = dot_nn(table, low_x[:, span])
        count = table.shape[0] // folds
        which = lax.shift_right_logical(cx, fold.bit_length() - 1)
        found = prod[(folds - 1) * count:]
        for f in range(folds - 1):
            found = jnp.where(which == f, prod[f * count:(f + 1) * count], found)
        z_w, z_d, z_x = summed(found[:4 * size_y], fx, *weights(size_y, cy, fy))
        y_w, y_d, y_x = summed(found[4 * size_y:], fx, *weights(size_z, cz, fz))
        (wz, dz), (wy, dy) = top(cz, fz, size_z), top(cy, fy, size_y)
        return by_four(
            base_s[0:1, span] + (dz * z_w + wy * y_d), base_s[1:2, span] + (wz * z_d + dy * y_w),
            base_s[2:3, span] + (wz * z_x + wy * y_x), 0.0)

    def about(span):
        cz, cy, cx, fz, fy, fx = place(span)
        (wz, dz), (wy, dy) = top(cz, fz, size_z), top(cy, fy, size_y)
        return by_four((slots[:, span] + 1).astype(F32), cx.astype(F32) + fx, wz * dy, wy * dz)

    def pack(values, into, terms):
        wide = 2 * group
        parts = [terms(jnp.concatenate([value] * 2, axis=0)) for value in values]

        def pack_group(g, carry):
            total = jnp.zeros((len(parts[0]) * wide, 2 * LANES), F32)
            for part, span in zip(parts, spans):
                mask = mine_s[:, span] if groups == 1 else own_rows(g, span, chunk)
                left = jnp.concatenate([each * mask[r:r + 16] for each in part for r in range(0, wide, 16)], axis=0)
                total = total + dot_nt(left, rank_s[:, span])
            packed = total[:wide]
            for k in range(1, len(parts[0])):
                packed = packed + total[k * wide:(k + 1) * wide]
            for d in range(group):
                half, side = d // 2, d % 2 * LANES
                into[g * group + d, 0:4] = packed[4 * half:4 * half + 4, side:side + LANES]
            return carry

        over(groups, pack_group, 0)

    pl.semaphore_wait(barrier, devices - 1)
    below_z = lax.rem(gz + count_z - 1, count_z)
    below_y = lax.rem(gy + count_y - 1, count_y)
    halos = []
    for i, (source, target, device) in enumerate((
        (row_s, halo_y, (gz, below_y)),
        (grid_v.at[0], halo_z, (below_z, gy)),
    )):
        halos.append(pltpu.make_async_remote_copy(
            src_ref=source, dst_ref=target, send_sem=halo_send.at[i], recv_sem=halo_recv.at[i],
            device_id=device, device_id_type=MESH,
        ))
        halos[-1].start()

    def send_all(source, target, send_sem, recv_sem):
        def post(to_z, to_y):
            pltpu.make_async_remote_copy(
                src_ref=source.at[to_z * count_y + to_y], dst_ref=target.at[me], send_sem=send_sem, recv_sem=recv_sem,
                device_id=(to_z, to_y), device_id_type=MESH,
            ).start()

        first = min(2, count_y)
        for to_y in range(first):
            pl.when(me != to_y)(lambda to_y=to_y: post(0, to_y))

        def post_later(to_z, to_y):
            pl.when(to_z * count_y + to_y >= first)(lambda: post(to_z, to_y))

        each_other(post_later)

    def sent(source, target, send_sem, recv_sem, count):
        at = pl.ds(0, count)
        return pltpu.make_async_remote_copy(
            src_ref=source.at[at], dst_ref=target.at[at], send_sem=send_sem, recv_sem=recv_sem,
            device_id=(below_z, below_y), device_id_type=MESH,
        )

    owner = owners[...]
    before = hot(iota((chunk, chunk), 0) < iota((chunk, chunk), 1))

    def rank_group(g, ranks):
        mine = jnp.where(iota((group, rows), 0) + g * group == owner, 1.0, 0.0)
        pieces = [mine[:, c * chunk:(c + 1) * chunk] for c in range(chunks)]
        inside = dot_nn(jnp.concatenate(pieces, axis=0).astype(BF), before)
        start = jnp.zeros((group, 1), F32)
        found = []
        for c in range(chunks):
            where = inside[c * group:(c + 1) * group] + start
            found.append(jnp.sum(pieces[c] * where, axis=0, keepdims=True))
            start = start + jnp.sum(pieces[c], axis=1, keepdims=True)
        return ranks + jnp.concatenate(found, axis=1)

    ranks = over(groups, rank_group, jnp.zeros((1, rows), F32))
    odd = lax.bitwise_and(owner, 1)
    rank_s[...] = hot(iota((2 * LANES, rows), 0) == ranks.astype(jnp.int32) + odd * LANES)

    def own_rows(g, span, count):
        whose = lax.shift_right_logical(iota((2 * group, count), 0), 2) + g * (group // 2)
        return hot(whose == lax.shift_right_logical(owners[:, span], 1))

    if groups == 1:
        mine_s[...] = own_rows(0, pl.ds(0, rows), rows)

    early = chunks // 2
    for span in spans[:early]:
        main_chunk(span)
    pack([about(span) for span in spans], early_s, thirds)
    shared = [corner[:, k * LANES:(k + 1) * LANES] for k in range(pieces_x)]

    def share(d, carry):
        for k in range(pieces_x):
            early_s[d, 4 + k:5 + k] = shared[k]
        return carry

    lax.fori_loop(0, devices, share, 0, unroll=devices <= 64)

    send_all(early_s, early_r, early_send, early_recv)
    early_r[me] = early_s[me]

    for span in spans[early:]:
        main_chunk(span)

    for copy in halos:
        copy.wait()
    table = folded([halo_z[...], halo_y[...]])
    pack([with_halos(table, span) for span in spans], later_s, split)
    send_all(later_s, later_r, later_send, later_recv.at[gz])
    later_r[me] = later_s[me]

    sent(early_s, early_r, early_send, early_recv, devices - 1).wait()

    def from_corner(source):
        info = early_r[source]
        at_z, at_y = source // count_y, source % count_y
        if isinstance(source, int):
            other = (at_z + 1) % count_z * count_y + (at_y + 1) % count_y
        else:
            other = lax.rem(at_z + 1, count_z) * count_y + lax.rem(at_y + 1, count_y)
        row = early_r[other][4:]
        row = jnp.concatenate([row, row], axis=0) if pieces_x == 4 else row
        full = row.shape[0]
        where_x = jnp.broadcast_to(info[1:2], (full, LANES))
        cell = where_x.astype(jnp.int32)
        frac = where_x - cell.astype(F32)
        part = lax.bitwise_and(iota((full, LANES), 0), pieces_x - 1)

        def read(at):
            found = jnp.take_along_axis(row, lax.bitwise_and(at, LANES - 1), axis=1, mode="promise_in_bounds")
            found = jnp.where(part == lax.shift_right_logical(at, 7), found, 0.0)
            return jnp.sum(found[:pieces_x], axis=0, keepdims=True)

        low, high = read(cell), read(lax.bitwise_and(cell + 1, size_x - 1))
        slope = high - low
        value = low + frac[0:1] * slope
        wz, wy = info[2:3], info[3:4]
        return by_four(wy * value, wz * value, wz * wy * slope, 0.0)[:4]

    def where_to(blocks):
        record = jnp.concatenate([block[0:1] for block in blocks], axis=1).astype(jnp.int32) - 1
        width = record.shape[1]
        which = lax.shift_right_logical(iota((4 * highs, width), 0), 2)
        return (hot(iota((LANES, width), 0) == lax.bitwise_and(record, LANES - 1)),
                hot(which == lax.shift_right_arithmetic(record, 7)))

    def added(blocks, low_hot, high_hot):
        values = jnp.concatenate(blocks, axis=1)
        halves = split(jnp.concatenate([values] * 4, axis=0))
        left = jnp.concatenate([half * high_hot[r:r + 16] for half in halves for r in range(0, 4 * highs, 16)], axis=0)
        total = dot_nt(left, low_hot)
        return total[:4 * highs] + total[4 * highs:]

    if groups == 1:
        low_hot, high_hot = where_to([early_r[d] for d in range(devices)])
        place_s[...] = low_hot
        high_s[...] = high_hot
        total = added([from_corner(d) for d in range(devices)], low_hot, high_hot)
    else:
        def corner_group(g, total):
            low_hot, high_hot = where_to([early_r[g * group + d] for d in range(group)])
            return total + added([from_corner(g * group + d) for d in range(group)], low_hot, high_hot)

        total = over(groups, corner_group, jnp.zeros((4 * highs, LANES), F32))

    for shift in [*range(1, count_z - 1), 0, *range(max(1, count_z - 1), count_z)]:
        from_z = lax.rem(gz + shift, count_z)
        sent(later_s, later_r, later_send, later_recv.at[from_z], count_y if shift else count_y - 1).wait_recv()
        if groups == 1:
            first = from_z * count_y
            width = count_y * LANES
            at = pl.ds(pl.multiple_of(first * LANES, width), width)
            total = total + added([later_r[first + d] for d in range(count_y)], place_s[:, at], high_s[:, at])
    sent(later_s, later_r, later_send, later_recv.at[gz], devices - 1).wait_send()
    if groups > 1:
        def add_group(g, total):
            low_hot, high_hot = where_to([early_r[g * group + d] for d in range(group)])
            return total + added([later_r[g * group + d] for d in range(group)], low_hot, high_hot)

        total = over(groups, add_group, total)
    for h in range(highs):
        out[:, h * LANES:(h + 1) * LANES] = total[4 * h:4 * h + 3]


def body(grid_grad, cells, offsets, owners, slots):
    size_z, size_y, size_x = grid_grad.shape
    rows = cells.shape[1]
    count_z = lax.axis_size("gz")
    devices = count_z * lax.axis_size("gy")
    group = min(32, devices)
    width = devices * LANES if devices == group else LANES
    vmem = pl.BlockSpec(memory_space=pltpu.VMEM)
    hbm = pl.BlockSpec(memory_space=pltpu.HBM)
    return pl.pallas_call(
        kernel,
        out_shape=pltpu.VMEM((3, rows), F32),
        in_specs=[hbm] * 5,
        out_specs=vmem,
        scratch_shapes=[
            pltpu.VMEM((3, rows), jnp.int32),
            pltpu.VMEM((3, rows), jnp.int32),
            pltpu.VMEM((1, rows), jnp.int32),
            pltpu.VMEM((1, rows), jnp.int32),
            pltpu.VMEM((size_z, size_y, size_x), F32),
            pltpu.VMEM((size_z, size_x), F32),
            pltpu.VMEM((size_y, size_x), F32),
            pltpu.VMEM((size_z, size_x), F32),
            pltpu.VMEM((4 * size_z * size_y, size_x), BF),
            pltpu.VMEM((min(256, size_x), rows), BF),
            pltpu.VMEM((8, rows), F32),
            pltpu.VMEM((2 * LANES, rows), BF),
            pltpu.VMEM((2 * group, rows), BF),
            pltpu.VMEM((devices, 4 + size_x // LANES, LANES), F32),
            pltpu.VMEM((devices, 4, LANES), F32),
            pltpu.VMEM((devices, 4 + size_x // LANES, LANES), F32),
            pltpu.VMEM((devices, 4, LANES), F32),
            pltpu.VMEM((LANES, width), BF),
            pltpu.VMEM((4 * rows // LANES, width), BF),
            pltpu.SemaphoreType.DMA((5,)),
            pltpu.SemaphoreType.DMA((2,)),
            pltpu.SemaphoreType.DMA((2,)),
            pltpu.SemaphoreType.DMA,
            pltpu.SemaphoreType.DMA,
            pltpu.SemaphoreType.DMA,
            pltpu.SemaphoreType.DMA((count_z,)),
        ],
        compiler_params=pltpu.CompilerParams(collective_id=0, has_side_effects=True, vmem_limit_bytes=56 * 1024 * 1024),
        name="cic",
    )(grid_grad, cells, offsets, owners.reshape(1, rows), slots.reshape(1, rows))


def solution(mesh):
    placed = (
        P("gz", "gy", None),
        P(None, ("gz", "gy")),
        P(None, ("gz", "gy")),
        P(("gz", "gy"), None),
        P(("gz", "gy")),
    )
    return jax.shard_map(
        body, mesh=mesh, in_specs=placed, out_specs=P(None, ("gz", "gy")), check_vma=False
    )
```

time: 18.7 us -> 16.6 us (0.89)
  Pallas kernels: 18.5 us -> 15.8 us
  local copies, waits for them, and re-layouts: 0 us -> 0.62 us
    pallas_call x2 -> x1, Pallas kernels: 18.5 us -> 15.8 us  [body(): pl.pallas_call(kernel, out_shape=pltpu.VMEM((3, rows), F32), in_specs=[hb...]
    unnamed x0 -> x1, local copies, waits for them, and re-layouts: none -> 0.62 us
where the time goes in v1:
time: 16.6 us; the launch traced here: 16.4 us
  Pallas kernels  15.8 us (95%)
  local copies, waits for them, and re-layouts  0.62 us (4%)
    pallas_call x1, Pallas kernels, body(): pl.pallas_call(kernel, out_shape=pltpu.VMEM((3, rows), F32), in_specs=[hb...  15.8 us
    unnamed x1, local copies, waits for them, and re-layouts  0.62 us

profile of v1, /device:TPU:0, one launch (start us, length us, event | category | flops | bytes accessed | tf_op | source)
XLA Modules:
  0.0 16.4 jit_solution(8030944277737490919)
XLA Ops:
  0.0 15.8 %cic.1 = f32[3,2048]{1,0:T(4,128)S(1)} custom-call(f32[16,16,512]{2,1,0:T(8,128)} %grid_ref.1, s32[3,2048]{1,0:T(4,128)} %cells_ref.1, s32[3,2048]{1,0:T(4,128)} %offsets_ref.1, s32[1,2048]{1,0:T(1,128)} %bitcast.2, s32[1,2048]{1,0:T(1,128)} %bitcast.3), custom_call_target="tpu_custom_call" | custom-call | tf_op jit(solution)/shard_map/cic/pallas_call | solution.py:377
  15.8 0.6 %copy.7 = f32[3,2048]{1,0:T(4,128)} copy(f32[3,2048]{1,0:T(4,128)S(1)} %cic.1) | data formatting | bytes 49152

commit v2 on v1

v2 whole, which is shorter than its diff:
```python
import jax
import jax.numpy as jnp
from jax import lax
from jax.experimental import pallas as pl
from jax.experimental.pallas import tpu as pltpu
from jax.sharding import PartitionSpec as P

MESH = pl.DeviceIdType.MESH
BF = jnp.bfloat16
F32 = jnp.float32
LANES = 128


def iota(shape, axis):
    return lax.broadcasted_iota(jnp.int32, shape, axis)


def hot(mask):
    return jnp.where(mask, 1.0, 0.0).astype(BF)


def split(value):
    high = value.astype(BF)
    low = (value - high.astype(F32)).astype(BF)
    return high, low


def dot_nn(a, b):
    return lax.dot_general(a, b, (((1,), (0,)), ((), ())), preferred_element_type=F32)


def dot_nt(a, b):
    return lax.dot_general(a, b, (((1,), (1,)), ((), ())), preferred_element_type=F32)


def with_diff(rows):
    size_x = rows.shape[1]
    diff = pltpu.roll(rows, size_x - 1, 1) - rows
    return jnp.concatenate([*split(rows), *split(diff)], axis=0)


def hot_at(size, value, shift=0):
    value = jnp.broadcast_to(value.astype(F32), (16, value.shape[1])).astype(BF)
    at = lax.shift_right_logical(iota(value.shape, 0), shift).astype(F32)
    one, none = jnp.ones(value.shape, BF), jnp.zeros(value.shape, BF)
    return jnp.concatenate(
        [jnp.where((at + float(k >> shift)).astype(BF) == value, one, none) for k in range(0, size, 16)], axis=0)


def thirds(value):
    high, rest = split(value)
    return high, rest, (value - high.astype(F32) - rest.astype(F32)).astype(BF)


def over(count, step, carry):
    if count == 1:
        return step(0, carry)
    return lax.fori_loop(0, count, step, carry)


def kernel(
    grid_ref, cells_ref, offsets_ref, owners_ref, slots_ref, out,
    cells, offsets, owners, slots, grid_v, row_s, halo_s, mesh_s, low_x, base_s, last_s, rank_s, rank_t, mine_s, early_s, later_s,
    first_s,
    early_r, later_r, place_s, high_s, load_sem, halo_send, halo_recv, early_send, early_recv, later_send, later_recv,
):
    count_z, count_y = lax.axis_size("gz"), lax.axis_size("gy")
    devices = count_z * count_y
    gz, gy = lax.axis_index("gz"), lax.axis_index("gy")
    me = gz * count_y + gy
    size_z, size_y, size_x = grid_ref.shape
    rows = cells.shape[1]
    chunk = min(256, rows)
    chunks = rows // chunk
    spans = [pl.ds(j * chunk, chunk) for j in range(chunks)]
    group = min(32, devices)
    groups = devices // group
    slab = size_z * size_y
    pieces_x = size_x // LANES
    fold = low_x.shape[0]
    folds = size_x // fold
    highs = rows // LANES

    loads = []
    for i, (source, target) in enumerate((
        (owners_ref, owners), (grid_ref, grid_v), (cells_ref, cells), (offsets_ref, offsets), (slots_ref, slots),
    )):
        loads.append(pltpu.make_async_copy(source, target, load_sem.at[i]))
        loads[-1].start()
    barrier = pltpu.get_barrier_semaphore()

    def each_other(act):
        few = devices <= 64

        def along_y(to_z, first):
            def step(shift, carry):
                act(to_z, lax.rem(gy + shift, count_y))
                return carry
            lax.fori_loop(first, count_y, step, 0, unroll=few)

        def step_z(shift, carry):
            along_y(lax.rem(gz + shift, count_z), 0)
            return carry
        along_y(gz, 1)
        lax.fori_loop(1, count_z, step_z, 0, unroll=few)

    def greet(to_z, to_y):
        pl.semaphore_signal(barrier, inc=1, device_id=(to_z, to_y), device_id_type=MESH)

    each_other(greet)

    loads[0].wait()
    owner = owners[...]
    before = hot(iota((chunk, chunk), 0) < iota((chunk, chunk), 1))

    def rank_group(g, ranks):
        mine = jnp.where(iota((group, rows), 0) + g * group == owner, 1.0, 0.0)
        pieces = [mine[:, c * chunk:(c + 1) * chunk] for c in range(chunks)]
        inside = dot_nn(jnp.concatenate(pieces, axis=0).astype(BF), before)
        start = jnp.zeros((group, 1), F32)
        found = []
        for c in range(chunks):
            where = inside[c * group:(c + 1) * group] + start
            found.append(jnp.sum(pieces[c] * where, axis=0, keepdims=True))
            start = start + jnp.sum(pieces[c], axis=1, keepdims=True)
        return ranks + jnp.concatenate(found, axis=1)

    ranks = over(groups, rank_group, jnp.zeros((1, rows), F32))
    odd = lax.bitwise_and(owner, 1)
    rank_s[...] = hot_at(2 * LANES, ranks + (odd * LANES).astype(F32))

    def own_rows(g, span):
        return hot_at(2 * group, lax.shift_right_logical(owners[:, span], 1) - g * (group // 2), 2)

    if groups == 1:
        mine_s[...] = own_rows(0, pl.ds(0, rows))

    for copy in loads[1:]:
        copy.wait()
    row_s[...] = grid_v[:, 0, :]
    mesh_s[...] = with_diff(grid_v[...].reshape(slab, size_x))
    corner = grid_v[0, 0:1, :]

    def place(span):
        cell = cells[:, span]
        frac = (offsets[:, span].astype(F32) + 0.5) / 1024.0
        return (cell[0:1] - gz * size_z, cell[1:2] - gy * size_y, cell[2:3],
                frac[0:1], frac[1:2], frac[2:3])

    def weights(size, cell, frac):
        at = iota((size, cell.shape[1]), 0)
        lower, upper = at == cell, at == cell + 1
        return (jnp.where(lower, 1.0 - frac, jnp.where(upper, frac, 0.0)),
                jnp.where(lower, -1.0, jnp.where(upper, 1.0, 0.0)))

    def by_four(first, second, third, fourth):
        part = lax.bitwise_and(iota((8, first.shape[1]), 0), 3)
        return jnp.where(part == 0, first, jnp.where(part == 1, second, jnp.where(part == 2, third, fourth)))

    def main_chunk(span):
        cz, cy, cx, fz, fy, fx = place(span)
        which, low = lax.shift_right_logical(cx, fold.bit_length() - 1), lax.bitwise_and(cx, fold - 1)
        low_x[:, span] = hot_at(fold, low)
        prod = dot_nn(mesh_s[...], jnp.concatenate(
            [hot_at(fold, jnp.where(which == f, low, -1)) for f in range(folds)], axis=0))
        z_at, z_frac = jnp.broadcast_to(cz, (8, chunk)), jnp.broadcast_to(fz, (8, chunk))
        gz0 = 1.0 - z_frac
        tiles = size_y // 8
        total = [[jnp.zeros((8, chunk), F32) for _ in range(tiles)] for _ in range(4)]
        for z in range(size_z):
            lower, upper = z_at == z, z_at == z - 1
            weight = jnp.where(lower, gz0, jnp.where(upper, z_frac, 0.0))
            diff = jnp.where(lower, -1.0, jnp.where(upper, 1.0, 0.0))
            for t in range(tiles):
                first = z * size_y + 8 * t
                at = [prod[q * slab + first:q * slab + first + 8] for q in range(4)]
                value, slope = at[0] + at[1], at[2] + at[3]
                total[0][t] += weight * value
                total[1][t] += diff * value
                total[2][t] += weight * slope
                total[3][t] += diff * slope
        w_y, d_y = weights(size_y, cy, fy)
        sums = [0.0, 0.0, 0.0]
        for t in range(tiles):
            a_w, a_d, b_w, b_d = (total[q][t] for q in range(4))
            w, d = w_y[8 * t:8 * t + 8], d_y[8 * t:8 * t + 8]
            sums = [sums[0] + (a_d + fx * b_d) * w, sums[1] + (a_w + fx * b_w) * d, sums[2] + b_w * w]
        for q in range(3):
            base_s[q, :, span] = sums[q]

    def top(cell, frac, size):
        at_top = cell == size - 1
        return jnp.where(at_top, frac, 0.0), jnp.where(at_top, 1.0, 0.0)

    def folded(plane):
        table = with_diff(plane)
        return jnp.concatenate([table[:, f * fold:(f + 1) * fold] for f in range(folds)], axis=0)

    def by_rows(first, second, third):
        row = iota(first.shape, 0)
        even, lower = lax.bitwise_and(row, 1) == 0, lax.bitwise_and(row, 2) == 0
        pair = jnp.where(even, first, second) + pltpu.roll(jnp.where(even, second, first), 1, 0)
        third = third + pltpu.roll(third, 1, 0)
        third = jnp.where(even, third, 0.0)
        both = jnp.where(lower, pair, third) + pltpu.roll(jnp.where(lower, third, pair), 2, 0)
        return both + pltpu.roll(both, 4, 0)

    def either(first, one, other):
        if isinstance(first, bool):
            return one if first else other
        return jnp.where(first, one, other)

    def halo_weights(span, along_y):
        cz, cy, cx, fz, fy, fx = place(span)
        size = either(along_y, size_y, size_z) if isinstance(along_y, bool) else size_y
        w, d = weights(size, either(along_y, cy, cz), either(along_y, fy, fz))
        w_top, d_top = top(either(along_y, cz, cy), either(along_y, fz, fy), either(along_y, size_z, size_y))
        across, beside = d_top * w, w_top * d
        return either(along_y, across, beside), either(along_y, beside, across), w_top * w

    def halo_sums(table, span, factors):
        cx, fx = place(span)[2::3]
        prod = dot_nn(table, low_x[:, span])
        count = table.shape[0] // folds
        size = count // 4
        which = lax.shift_right_logical(cx, fold.bit_length() - 1)

        def found(first):
            pick = None
            for f in reversed(range(folds)):
                at = f * count + first
                part = prod[at:at + size] + prod[at + size:at + 2 * size]
                pick = part if pick is None else jnp.where(which == f, part, pick)
            return pick

        value, slope = found(0), found(2 * size)
        read = value + fx * slope
        parts = (factors[0] * read, factors[1] * read, factors[2] * slope)
        sums = []
        for q in range(3):
            total = base_s[q, :, span]
            for t in range(0, size, 8):
                total = total + parts[q][t:t + 8]
            sums.append(total)
        return sums

    def about(span):
        cz, cy, cx, fz, fy, fx = place(span)
        (wz, dz), (wy, dy) = top(cz, fz, size_z), top(cy, fy, size_y)
        return by_four((slots[:, span] + 1).astype(F32), cx.astype(F32) + fx, wz * dy, wy * dz)

    def pack_rows(g, parts, wide, ranked):
        total = jnp.zeros((len(parts[0]) * wide, 2 * LANES), F32)
        for part, span in zip(parts, spans):
            mask = mine_s[:, span] if groups == 1 else own_rows(g, span)
            left = jnp.concatenate([each * mask[r:r + 16] for each in part for r in range(0, wide, 16)], axis=0)
            total = total + ranked(left, span)
        packed = total[:wide]
        for k in range(1, len(parts[0])):
            packed = packed + total[k * wide:(k + 1) * wide]
        return packed

    def keep(packed, into, first):
        for d in range(packed.shape[0] // 2):
            half, side = d // 2, d % 2 * LANES
            into[first + d, 0:4] = packed[4 * half:4 * half + 4, side:side + LANES]

    def pack(parts, into, ranked):
        def pack_group(g, carry):
            keep(pack_rows(g, parts, 2 * group, ranked), into, g * group)
            return carry

        over(groups, pack_group, 0)

    def by_rank(left, span):
        return dot_nt(left, rank_s[:, span])

    def by_rank_t(left, span):
        return dot_nn(left, rank_t[span])

    def terms_of(value, terms):
        return terms(jnp.concatenate([value] * 2, axis=0))

    pl.semaphore_wait(barrier, devices - 1)
    below_z = lax.rem(gz + count_z - 1, count_z)
    below_y = lax.rem(gy + count_y - 1, count_y)
    halos = []
    for i, (source, target, device) in enumerate((
        (row_s, halo_s.at[0, 0:size_z], (gz, below_y)),
        (grid_v.at[0], halo_s.at[1, 0:size_y], (below_z, gy)),
    )):
        halos.append(pltpu.make_async_remote_copy(
            src_ref=source, dst_ref=target, send_sem=halo_send.at[i], recv_sem=halo_recv.at[i],
            device_id=device, device_id_type=MESH,
        ))
        halos[-1].start()

    def post(source, target, send_sem, recv_sem, device):
        pltpu.make_async_remote_copy(
            src_ref=source, dst_ref=target.at[me], send_sem=send_sem, recv_sem=recv_sem,
            device_id=device, device_id_type=MESH,
        ).start()

    first_few = min(2, count_y)

    def post_first(source, *where):
        for to_y in range(first_few):
            pl.when(me != to_y)(lambda to_y=to_y: post(source.at[to_y], *where, (0, to_y)))

    def post_rest(source, *where):
        def one(to_z, to_y):
            other = to_z * count_y + to_y
            pl.when(other >= first_few)(lambda: post(source.at[other], *where, (to_z, to_y)))

        each_other(one)

    def sent(source, target, send_sem, recv_sem, count):
        at = pl.ds(0, count)
        return pltpu.make_async_remote_copy(
            src_ref=source.at[at], dst_ref=target.at[at], send_sem=send_sem, recv_sem=recv_sem,
            device_id=(below_z, below_y), device_id_type=MESH,
        )

    early = chunks // 2
    for span in spans[:early]:
        main_chunk(span)
    pack([terms_of(about(span), thirds) for span in spans], early_s, by_rank)
    shared = [corner[:, k * LANES:(k + 1) * LANES] for k in range(pieces_x)]

    def share(d, carry):
        for k in range(pieces_x):
            early_s[d, 4 + k:5 + k] = shared[k]
        return carry

    lax.fori_loop(0, devices, share, 0, unroll=devices <= 64)

    post_first(early_s, early_r, early_send, early_recv)
    post_rest(early_s, early_r, early_send, early_recv)
    early_r[me] = early_s[me]

    for span in spans:
        rank_t[span] = rank_s[:, span].T
    for span in spans[early:]:
        main_chunk(span)

    at_end = lax.div(gy + 1, count_y)
    y_last = at_end == 1 if size_z == size_y else True
    y_copy, z_copy = halos

    def wait_for(first):
        if isinstance(first, bool):
            (z_copy if first else y_copy).wait()
        else:
            pl.when(first)(z_copy.wait)
            pl.when(jnp.logical_not(first))(y_copy.wait)

    def plane(along_y):
        if isinstance(along_y, bool):
            return folded(halo_s[1, 0:size_y] if along_y else halo_s[0, 0:size_z])
        return folded(halo_s[at_end if along_y is y_last else 1 - at_end])

    y_first = not y_last if isinstance(y_last, bool) else jnp.logical_not(y_last)
    wait_for(y_last)
    table = plane(y_last)
    for span in spans:
        sums = halo_sums(table, span, halo_weights(span, y_last))
        for q in range(3):
            base_s[q, :, span] = sums[q]
        for q, factor in enumerate(halo_weights(span, y_first)):
            last_s[q, :, span] = factor
    wait_for(y_first)
    table = plane(y_first)
    parts = [
        terms_of(by_rows(*halo_sums(table, span, [last_s[q, :, span] for q in range(3)])), split) for span in spans
    ]
    keep(pack_rows(0, parts, 16, by_rank_t), first_s, 0)
    post_first(first_s, later_r, later_send, later_recv.at[lax.div(gy, 2)])
    pack(parts, later_s, by_rank_t)
    post_rest(later_s, later_r, later_send, later_recv.at[lax.div(gy, 2)])
    later_r[me] = later_s[me]

    sent(early_s, early_r, early_send, early_recv, devices - 1).wait()

    def from_corner(source):
        info = early_r[source]
        at_z, at_y = source // count_y, source % count_y
        if isinstance(source, int):
            other = (at_z + 1) % count_z * count_y + (at_y + 1) % count_y
        else:
            other = lax.rem(at_z + 1, count_z) * count_y + lax.rem(at_y + 1, count_y)
        row = early_r[other][4:]
        row = jnp.concatenate([row, row], axis=0) if pieces_x == 4 else row
        full = row.shape[0]
        where_x = jnp.broadcast_to(info[1:2], (full, LANES))
        cell = where_x.astype(jnp.int32)
        frac = where_x - cell.astype(F32)
        part = lax.bitwise_and(iota((full, LANES), 0), pieces_x - 1)

        def read(at):
            found = jnp.take_along_axis(row, lax.bitwise_and(at, LANES - 1), axis=1, mode="promise_in_bounds")
            found = jnp.where(part == lax.shift_right_logical(at, 7), found, 0.0)
            return jnp.sum(found[:pieces_x], axis=0, keepdims=True)

        low, high = read(cell), read(lax.bitwise_and(cell + 1, size_x - 1))
        slope = high - low
        value = low + frac[0:1] * slope
        wz, wy = info[2:3], info[3:4]
        return by_four(wy * value, wz * value, wz * wy * slope, 0.0)[:4]

    def where_to(blocks):
        record = jnp.concatenate([block[0:1] for block in blocks], axis=1).astype(jnp.int32) - 1
        return (hot_at(LANES, lax.bitwise_and(record, LANES - 1)),
                hot_at(4 * highs, lax.shift_right_arithmetic(record, 7), 2))

    def added(blocks, low_hot, high_hot):
        values = jnp.concatenate(blocks, axis=1)
        halves = split(jnp.concatenate([values] * 4, axis=0))
        left = jnp.concatenate([half * high_hot[r:r + 16] for half in halves for r in range(0, 4 * highs, 16)], axis=0)
        total = dot_nt(left, low_hot)
        return total[:4 * highs] + total[4 * highs:]

    order = [z * count_y + y for first in range(0, count_y, 2) for z in range(count_z) for y in (first, first + 1)]
    if groups == 1:
        low_hot, high_hot = where_to([early_r[d] for d in order])
        place_s[...] = low_hot
        high_s[...] = high_hot
        total = added([from_corner(d) for d in order], low_hot, high_hot)
    else:
        def corner_group(g, total):
            low_hot, high_hot = where_to([early_r[g * group + d] for d in range(group)])
            return total + added([from_corner(g * group + d) for d in range(group)], low_hot, high_hot)

        total = over(groups, corner_group, jnp.zeros((4 * highs, LANES), F32))

    batch = 2 * count_z
    for part in range(count_y // 2):
        def wait_for_batch(count):
            sent(later_s, later_r, later_send, later_recv.at[part], count).wait_recv()

        pl.when(lax.div(gy, 2) == part)(lambda: wait_for_batch(batch - 1))
        pl.when(lax.div(gy, 2) != part)(lambda: wait_for_batch(batch))
        if groups == 1:
            at = slice(part * batch * LANES, (part + 1) * batch * LANES)
            sources = order[part * batch:(part + 1) * batch]
            total = total + added([later_r[d] for d in sources], place_s[:, at], high_s[:, at])
    sent(later_s, later_r, later_send, later_recv.at[0], devices - 1).wait_send()
    if groups > 1:
        def add_group(g, total):
            low_hot, high_hot = where_to([early_r[g * group + d] for d in range(group)])
            return total + added([later_r[g * group + d] for d in range(group)], low_hot, high_hot)

        total = over(groups, add_group, total)
    for h in range(highs):
        out[:, h * LANES:(h + 1) * LANES] = total[4 * h:4 * h + 3]


def body(grid_grad, cells, offsets, owners, slots):
    size_z, size_y, size_x = grid_grad.shape
    rows = cells.shape[1]
    count_y = lax.axis_size("gy")
    devices = lax.axis_size("gz") * count_y
    group = min(32, devices)
    width = devices * LANES if devices == group else LANES
    vmem = pl.BlockSpec(memory_space=pltpu.VMEM)
    hbm = pl.BlockSpec(memory_space=pltpu.HBM)
    return pl.pallas_call(
        kernel,
        out_shape=pltpu.VMEM((3, rows), F32),
        in_specs=[hbm] * 5,
        out_specs=vmem,
        scratch_shapes=[
            pltpu.VMEM((3, rows), jnp.int32),
            pltpu.VMEM((3, rows), jnp.int32),
            pltpu.VMEM((1, rows), jnp.int32),
            pltpu.VMEM((1, rows), jnp.int32),
            pltpu.VMEM((size_z, size_y, size_x), F32),
            pltpu.VMEM((size_z, size_x), F32),
            pltpu.VMEM((2, max(size_z, size_y), size_x), F32),
            pltpu.VMEM((4 * size_z * size_y, size_x), BF),
            pltpu.VMEM((min(256, size_x), rows), BF),
            pltpu.VMEM((3, 8, rows), F32),
            pltpu.VMEM((3, size_z, rows), F32),
            pltpu.VMEM((2 * LANES, rows), BF),
            pltpu.VMEM((rows, 2 * LANES), BF),
            pltpu.VMEM((2 * group, rows), BF),
            pltpu.VMEM((devices, 4 + size_x // LANES, LANES), F32),
            pltpu.VMEM((devices, 4, LANES), F32),
            pltpu.VMEM((8, 4, LANES), F32),
            pltpu.VMEM((devices, 4 + size_x // LANES, LANES), F32),
            pltpu.VMEM((devices, 4, LANES), F32),
            pltpu.VMEM((LANES, width), BF),
            pltpu.VMEM((4 * rows // LANES, width), BF),
            pltpu.SemaphoreType.DMA((5,)),
            pltpu.SemaphoreType.DMA((2,)),
            pltpu.SemaphoreType.DMA((2,)),
            pltpu.SemaphoreType.DMA,
            pltpu.SemaphoreType.DMA,
            pltpu.SemaphoreType.DMA,
            pltpu.SemaphoreType.DMA((count_y // 2,)),
        ],
        compiler_params=pltpu.CompilerParams(collective_id=0, has_side_effects=True, vmem_limit_bytes=56 * 1024 * 1024),
        name="cic",
    )(grid_grad, cells, offsets, owners.reshape(1, rows), slots.reshape(1, rows))


def solution(mesh):
    placed = (
        P("gz", "gy", None),
        P(None, ("gz", "gy")),
        P(None, ("gz", "gy")),
        P(("gz", "gy"), None),
        P(("gz", "gy")),
    )
    return jax.shard_map(
        body, mesh=mesh, in_specs=placed, out_specs=P(None, ("gz", "gy")), check_vma=False
    )
```

time: 16.6 us -> 16.1 us (0.970)
  Pallas kernels: 15.8 us -> 15.2 us
    pallas_call x1, Pallas kernels: 15.8 us -> 15.2 us  [body(): pl.pallas_call(kernel, out_shape=pltpu.VMEM((3, rows), F32), in_specs=[hb...]
where the time goes in v2:
time: 16.1 us; the launch traced here: 15.9 us
  Pallas kernels  15.2 us (94%)
  local copies, waits for them, and re-layouts  0.62 us (4%)
    pallas_call x1, Pallas kernels, body(): pl.pallas_call(kernel, out_shape=pltpu.VMEM((3, rows), F32), in_specs=[hb...  15.2 us
    unnamed x1, local copies, waits for them, and re-layouts  0.62 us

profile of v2, /device:TPU:0, one launch (start us, length us, event | category | flops | bytes accessed | tf_op | source)
XLA Modules:
  0.0 15.9 jit_solution(3179628557385195401)
XLA Ops:
  0.0 15.2 %cic.1 = f32[3,2048]{1,0:T(4,128)S(1)} custom-call(f32[16,16,512]{2,1,0:T(8,128)} %grid_ref.1, s32[3,2048]{1,0:T(4,128)} %cells_ref.1, s32[3,2048]{1,0:T(4,128)} %offsets_ref.1, s32[1,2048]{1,0:T(1,128)} %bitcast.2, s32[1,2048]{1,0:T(1,128)} %bitcast.3), custom_call_target="tpu_custom_call" | custom-call | tf_op jit(solution)/shard_map/cic/pallas_call | solution.py:466
  15.2 0.6 %copy.7 = f32[3,2048]{1,0:T(4,128)} copy(f32[3,2048]{1,0:T(4,128)S(1)} %cic.1) | data formatting | bytes 49152

commit v3 on v2

--- a/solution.py
+++ b/solution.py
@@ -160,7 +160,7 @@
     def main_chunk(span):
         cz, cy, cx, fz, fy, fx = place(span)
         which, low = lax.shift_right_logical(cx, fold.bit_length() - 1), lax.bitwise_and(cx, fold - 1)
-        low_x[:, span] = hot_at(fold, low)
+        low_x[:, span] = hot_at(fold, low).astype(low_x.dtype)
         prod = dot_nn(mesh_s[...], jnp.concatenate(
             [hot_at(fold, jnp.where(which == f, low, -1)) for f in range(folds)], axis=0))
         z_at, z_frac = jnp.broadcast_to(cz, (8, chunk)), jnp.broadcast_to(fz, (8, chunk))
@@ -339,7 +339,7 @@
     early_r[me] = early_s[me]
 
     for span in spans:
-        rank_t[span] = rank_s[:, span].T
+        rank_t[span] = rank_s[:, span].T.astype(rank_t.dtype)
     for span in spans[early:]:
         main_chunk(span)
 
@@ -477,11 +477,11 @@
             pltpu.VMEM((size_z, size_x), F32),
             pltpu.VMEM((2, max(size_z, size_y), size_x), F32),
             pltpu.VMEM((4 * size_z * size_y, size_x), BF),
-            pltpu.VMEM((min(256, size_x), rows), BF),
+            pltpu.VMEM((min(256, size_x), rows), jnp.float8_e4m3fn),
             pltpu.VMEM((3, 8, rows), F32),
             pltpu.VMEM((3, size_z, rows), F32),
             pltpu.VMEM((2 * LANES, rows), BF),
-            pltpu.VMEM((rows, 2 * LANES), BF),
+            pltpu.VMEM((rows, 2 * LANES), jnp.float8_e4m3fn),
             pltpu.VMEM((2 * group, rows), BF),
             pltpu.VMEM((devices, 4 + size_x // LANES, LANES), F32),
             pltpu.VMEM((devices, 4, LANES), F32),

time: 16.1 us -> 15.9 us (0.988)
  no operation moved by 1% of the time
where the time goes in v3:
time: 15.9 us; the launch traced here: 15.7 us
  Pallas kernels  15.1 us (95%)
  local copies, waits for them, and re-layouts  0.62 us (4%)
    pallas_call x1, Pallas kernels, body(): pl.pallas_call(kernel, out_shape=pltpu.VMEM((3, rows), F32), in_specs=[hb...  15.1 us
    unnamed x1, local copies, waits for them, and re-layouts  0.62 us

profile of v3, /device:TPU:0, one launch (start us, length us, event | category | flops | bytes accessed | tf_op | source)
XLA Modules:
  0.0 15.7 jit_solution(11672090723718993161)
XLA Ops:
  0.0 15.1 %cic.1 = f32[3,2048]{1,0:T(4,128)S(1)} custom-call(f32[16,16,512]{2,1,0:T(8,128)} %grid_ref.1, s32[3,2048]{1,0:T(4,128)} %cells_ref.1, s32[3,2048]{1,0:T(4,128)} %offsets_ref.1, s32[1,2048]{1,0:T(1,128)} %bitcast.2, s32[1,2048]{1,0:T(1,128)} %bitcast.3), custom_call_target="tpu_custom_call" | custom-call | tf_op jit(solution)/shard_map/cic/pallas_call | solution.py:466
  15.1 0.6 %copy.7 = f32[3,2048]{1,0:T(4,128)} copy(f32[3,2048]{1,0:T(4,128)S(1)} %cic.1) | data formatting | bytes 49152

commit v4 on v3

--- a/solution.py
+++ b/solution.py
@@ -422,7 +422,7 @@
     order = [z * count_y + y for first in range(0, count_y, 2) for z in range(count_z) for y in (first, first + 1)]
     if groups == 1:
         low_hot, high_hot = where_to([early_r[d] for d in order])
-        place_s[...] = low_hot
+        place_s[...] = low_hot.astype(place_s.dtype)
         high_s[...] = high_hot
         total = added([from_corner(d) for d in order], low_hot, high_hot)
     else:
@@ -488,7 +488,7 @@
             pltpu.VMEM((8, 4, LANES), F32),
             pltpu.VMEM((devices, 4 + size_x // LANES, LANES), F32),
             pltpu.VMEM((devices, 4, LANES), F32),
-            pltpu.VMEM((LANES, width), BF),
+            pltpu.VMEM((LANES, width), jnp.float8_e4m3fn),
             pltpu.VMEM((4 * rows // LANES, width), BF),
             pltpu.SemaphoreType.DMA((5,)),
             pltpu.SemaphoreType.DMA((2,)),

time: 15.9 us -> 15.9 us (level)
  no operation moved by 1% of the time
where the time goes in v4:
time: 15.9 us; the launch traced here: 15.7 us
  Pallas kernels  15.1 us (95%)
  local copies, waits for them, and re-layouts  0.62 us (4%)
    pallas_call x1, Pallas kernels, body(): pl.pallas_call(kernel, out_shape=pltpu.VMEM((3, rows), F32), in_specs=[hb...  15.1 us
    unnamed x1, local copies, waits for them, and re-layouts  0.62 us

profile of v4, /device:TPU:0, one launch (start us, length us, event | category | flops | bytes accessed | tf_op | source)
XLA Modules:
  0.0 15.7 jit_solution(11829832072063542485)
XLA Ops:
  0.0 15.1 %cic.1 = f32[3,2048]{1,0:T(4,128)S(1)} custom-call(f32[16,16,512]{2,1,0:T(8,128)} %grid_ref.1, s32[3,2048]{1,0:T(4,128)} %cells_ref.1, s32[3,2048]{1,0:T(4,128)} %offsets_ref.1, s32[1,2048]{1,0:T(1,128)} %bitcast.2, s32[1,2048]{1,0:T(1,128)} %bitcast.3), custom_call_target="tpu_custom_call" | custom-call | tf_op jit(solution)/shard_map/cic/pallas_call | solution.py:466
  15.1 0.6 %copy.7 = f32[3,2048]{1,0:T(4,128)} copy(f32[3,2048]{1,0:T(4,128)S(1)} %cic.1) | data formatting | bytes 49152
